TPU v7x, 32 devices: a whole 2x2x4 slice. The times are simulated.
32 devices in a mesh: tok: 4 (over z), hid: 8 (over y, x, core).
Axes of the slice: x: 2, y: 2, z: 4, core: 2. Of those that a mesh axis runs over, the one named last changes fastest.
Arguments:
- tokens: bfloat16 [512, 4096], P('tok', 'hid'), may hold values from -6 to 6
- out_grad: bfloat16 [512, 4096], P('tok', 'hid'), may hold values from -6 to 6
- routing_ids: int32 [512, 2], P('tok'), may hold values from 0 to 3, all different within a row; in each aligned block of 128 rows (0 to 127, 128 to 255, ...) at most 96 rows name the same one
- route_weights: bfloat16 [512, 2], P('tok'), may hold values from 0.049804688 to 1
- gate_matrix: bfloat16 [4, 4096, 8192], P('tok', None, 'hid'), may hold values from -0.125 to 0.125
- up_matrix: bfloat16 [4, 4096, 8192], P('tok', None, 'hid'), may hold values from -0.09375 to 0.09375
- down_matrix: bfloat16 [4, 8192, 4096], P('tok', 'hid'), may hold values from -0.0625 to 0.0625
Outputs:
- input_grad: bfloat16 [512, 4096], P('tok', 'hid')
- route_grad: bfloat16 [512, 2], P('tok')
- gate_matrix_grad: bfloat16 [4, 4096, 8192], P('tok', None, 'hid')
- up_matrix_grad: bfloat16 [4, 4096, 8192], P('tok', None, 'hid')
- down_matrix_grad: bfloat16 [4, 8192, 4096], P('tok', 'hid')
Inputs may be any that keep to these rules, and one draw needn't show every extreme that they name: `routing_ids`: each token names two different experts. Among the 128 tokens of one index of tok no expert is named more than 96 times, a bound that some expert reaches in each such block.
All inputs are finite; a program needn't handle non-finite values.
Results may differ from a plain program's by a relative error of at most 0.0076.
Values may be sent and summed in bfloat16 or wider, within the bound.
A program may use at most 128 MiB of HBM per device.

v0:
```python
import jax
import jax.numpy as jnp
from jax import lax
from jax.sharding import PartitionSpec as P


def contract(left, right, left_dim, right_dim):
    return lax.dot_general(
        left, right, (((left_dim,), (right_dim,)), ((), ())), preferred_element_type=jnp.float32
    )


def per_device(tokens, out_grad, routing_ids, route_weights, gate_matrix, up_matrix, down_matrix):
    groups = lax.axis_size("tok")
    tok_rows = tokens.shape[0]
    capacity = 3 * tok_rows // groups
    flat = routing_ids.reshape(-1)
    choices = flat.shape[0]
    onehot = (flat[:, None] == jnp.arange(groups, dtype=jnp.int32)[None, :]).astype(jnp.int32)
    position = jnp.sum((jnp.cumsum(onehot, axis=0) - onehot) * onehot, axis=1)
    slots = flat * capacity + position
    source = (
        jnp.full((groups * capacity,), choices, jnp.int32)
        .at[slots]
        .set(jnp.arange(choices, dtype=jnp.int32))
    )
    valid = source < choices
    clipped = jnp.minimum(source, choices - 1)
    token_row = clipped // 2
    slot_weight = jnp.where(valid, route_weights.reshape(-1)[clipped], jnp.zeros((), jnp.bfloat16))

    def pack(rows):
        return jnp.where(valid[:, None], rows[token_row], jnp.zeros((), rows.dtype))

    slice_in, slice_grad, rows_weight = (
        lax.all_to_all(pack(tokens), "tok", split_axis=0, concat_axis=0, tiled=True),
        lax.all_to_all(pack(out_grad), "tok", split_axis=0, concat_axis=0, tiled=True),
        lax.all_to_all(slot_weight, "tok", split_axis=0, concat_axis=0, tiled=True),
    )
    rows_in, rows_grad = (
        lax.all_gather(slice_in, "hid", axis=1, tiled=True),
        lax.all_gather(slice_grad, "hid", axis=1, tiled=True),
    )
    gate_w = gate_matrix[0]
    up_w = up_matrix[0]
    down_w = down_matrix[0]
    gate = contract(rows_in, gate_w, 1, 0)
    upper = contract(rows_in, up_w, 1, 0)
    sig = jax.nn.sigmoid(gate)
    act = gate * sig
    weight_col = rows_weight.astype(jnp.float32)[:, None]
    hidden = (act * upper).astype(jnp.bfloat16)
    scaled = (act * upper * weight_col).astype(jnp.bfloat16)
    back = contract(rows_grad, down_w, 1, 1)
    route_local = jnp.sum(hidden.astype(jnp.float32) * back, axis=1)
    back_scaled = back * weight_col
    up_delta = (back_scaled * act).astype(jnp.bfloat16)
    gate_delta = (back_scaled * upper * sig * (1.0 + gate * (1.0 - sig))).astype(jnp.bfloat16)
    gate_out = contract(rows_in, gate_delta, 0, 0).astype(jnp.bfloat16)
    up_out = contract(rows_in, up_delta, 0, 0).astype(jnp.bfloat16)
    down_out = contract(scaled, rows_grad, 0, 0).astype(jnp.bfloat16)
    shares = lax.psum_scatter(
        contract(gate_w, gate_delta, 1, 1) + contract(up_w, up_delta, 1, 1),
        "hid",
        scatter_dimension=0,
        tiled=True,
    )
    route_total = lax.psum(route_local, "hid")
    back_rows, back_route = (
        lax.all_to_all(shares.astype(jnp.bfloat16), "tok", split_axis=1, concat_axis=1, tiled=True),
        lax.all_to_all(
            route_total.astype(jnp.bfloat16)[None, :],
            "tok",
            split_axis=1,
            concat_axis=1,
            tiled=True,
        ),
    )
    picked = jnp.take(back_rows, slots, axis=1).astype(jnp.float32)
    features = picked.shape[0]
    input_grad = jnp.sum(picked.reshape(features, tok_rows, 2), axis=2).T.astype(jnp.bfloat16)
    route_grad = jnp.take(back_route[0], slots).reshape(tok_rows, 2)
    return (input_grad, route_grad, gate_out[None], up_out[None], down_out[None])


def solution(mesh):
    in_specs = (
        P("tok", "hid"),
        P("tok", "hid"),
        P("tok", None),
        P("tok", None),
        P("tok", None, "hid"),
        P("tok", None, "hid"),
        P("tok", "hid", None),
    )
    out_specs = (
        P("tok", "hid"),
        P("tok", None),
        P("tok", None, "hid"),
        P("tok", None, "hid"),
        P("tok", "hid", None),
    )
    return jax.shard_map(
        per_device, mesh=mesh, in_specs=in_specs, out_specs=out_specs, check_vma=False
    )
```

profile of v0, /device:TPU:0, one launch (start us, length us, event | category | flops | bytes accessed | tf_op | source)
XLA Modules:
  0.0 222.8 jit_solution(9728812527769227037)
XLA Ops:
  11.1 1.4 scatter_custom_fusion
  12.6 2.7 %gather_fusion.1 = bf16[384]{0:T(512)(128)(2,1)S(1)} fusion(bf16[256]{0:T(256)(128)(2,1)S(1)} %reshape.111, s32[1024]{0:T(1024)S(1)} %get-tuple-element.31), kind=kCustom, calls=%fused_computation.1 | custom fusion | bytes 3072 | tf_op jit(solution)/shard_map/gather | solution.py:30
  15.4 2.1 gather_fusion.2
  17.5 2.1 gather_fusion
  19.7 17.9 %all_to_all.50 = bf16[4,96,512]{2,1,0:T(8,128)(2,1)} all-to-all(bf16[4,96,512]{2,1,0:T(8,128)(2,1)S(1)} %get-tuple-element.30), channel_id=1, replica_groups=mesh['tok'=4,'hid'=8] {'tok'}, dimensions={0} | all-to-all | bytes 786432 | tf_op jit(solution)/shard_map/all_to_all | solution.py:36
  37.7 13.9 %all_to_all.51 = bf16[4,96,512]{2,1,0:T(8,128)(2,1)} all-to-all(bf16[4,96,512]{2,1,0:T(8,128)(2,1)S(1)} %get-tuple-element.29), channel_id=1, replica_groups=mesh['tok'=4,'hid'=8] {'tok'}, dimensions={0} | all-to-all | bytes 786432 | tf_op jit(solution)/shard_map/all_to_all | solution.py:37
  51.8 8.1 %all_to_all.52 = bf16[4,96,1]{1,2,0:T(2,128)(2,1)S(1)} all-to-all(bf16[4,96,1]{1,2,0:T(2,128)(2,1)S(1)} %all_to_all.43), channel_id=1, replica_groups=mesh['tok'=4,'hid'=8] {'tok'}, dimensions={0} | all-to-all | bytes 1536 | tf_op jit(solution)/shard_map/all_to_all | solution.py:38
  60.0 9.6 %all-gather.5.cloned.1.call-done = bf16[384,4096]{1,0:T(8,128)(2,1)} async-done(((bf16[384,512]{1,0:T(8,128)(2,1)}), bf16[384,4096]{1,0:T(8,128)(2,1)}) %all-gather.5.cloned.1.call-update) | async-done | bytes 3145744 | tf_op jit(solution)/shard_map/all_gather | solution.py:41
  69.6 9.0 %fusion.2 = f32[384,1024]{1,0:T(8,128)} fusion(bf16[384,4096]{1,0:T(8,128)(2,1)} %all-gather.5.cloned.1.call-done, bf16[1,4096,1024]{2,1,0:T(8,128)(2,1)} %param.11), kind=kOutput, calls=%fused_computation.8 | convolution fusion | flops 3221225472 | bytes 13107200 | tf_op jit(solution)/shard_map/dot_general | solution.py:8
  78.6 7.1 %fusion.6 = f32[384,1024]{1,0:T(8,128)} fusion(bf16[384,4096]{1,0:T(8,128)(2,1)S(1)} %copy-done.3, bf16[1,4096,1024]{2,1,0:T(8,128)(2,1)} %param.12), kind=kOutput, calls=%fused_computation.12 | convolution fusion | flops 3221225472 | bytes 13107200 | tf_op jit(solution)/shard_map/dot_general | solution.py:8
  85.8 18.5 %all-gather.3.cloned.1.call-done = bf16[384,4096]{1,0:T(8,128)(2,1)} async-done(((bf16[384,512]{1,0:T(8,128)(2,1)}), bf16[384,4096]{1,0:T(8,128)(2,1)}) %all-gather.3.cloned.1.call-update) | async-done | bytes 3145744 | tf_op jit(solution)/shard_map/all_gather | solution.py:42
  104.2 9.4 %multiply_reduce_fusion = (f32[384]{0:T(512)S(1)}, bf16[384,1024]{1,0:T(8,128)(2,1)S(1)}, bf16[384,1024]{1,0:T(8,128)(2,1)S(1)}) fusion(f32[384,1024]{1,0:T(8,128)} %fusion.6, f32[384,1024]{1,0:T(8,128)} %fusion.2, f32[384]{0:T(512)S(1)} %reshape.112, bf16[384,4096]{1,0:T(8,128)(2,1)} %all-gather.3.cloned.1.call-done, bf16[1,1024,4096]{2,1,0:T(8,128)(2,1)} %param.13), kind=kOutput, calls=%fused_computation.21 | convolution fusion | flops 3228696064 | bytes 16256000 | tf_op jit(solution)/shard_map/dot_general | solution.py:8
  113.7 11.5 %fusion = f32[384,4096]{1,0:T(8,128)} fusion(bf16[384,1024]{1,0:T(8,128)(2,1)S(1)} %get-tuple-element.25, bf16[1,4096,1024]{2,1,0:T(8,128)(2,1)} %param.11), kind=kOutput, calls=%fused_computation.6 | convolution fusion | flops 3221225472 | bytes 15466496 | tf_op jit(solution)/shard_map/dot_general | solution.py:8
  125.2 7.3 %add_bitcast_fusion = f32[4096,384]{0,1:T(8,128)} fusion(f32[384,4096]{1,0:T(8,128)} %fusion, bf16[384,1024]{1,0:T(8,128)(2,1)S(1)} %get-tuple-element.26, bf16[1,4096,1024]{2,1,0:T(8,128)(2,1)S(1)} %bitcast.79), kind=kOutput, calls=%fused_computation.19 | convolution fusion | flops 3222798336 | bytes 21757952 | tf_op jit(solution)/shard_map/dot_general | solution.py:8
  132.7 13.1 %psum.7 = bf16[384]{0:T(512)(128)(2,1)S(1)} all-reduce(f32[384]{0:T(512)S(1)} %get-tuple-element.24), channel_id=1, replica_groups=mesh['tok'=4,'hid'=8] {'hid'}, use_global_device_ids=true, to_apply=%region_7.8 | all-reduce | flops 384 | bytes 2304 | tf_op jit(solution)/shard_map/psum | solution.py:68
  146.4 4.6 %all-to-all-start.4 = ((bf16[1,4,96]{2,0,1:T(2,128)(2,1)}), bf16[1,4,96]{2,0,1:T(2,128)(2,1)S(1)}, u32[]{:S(2)}, u32[]{:S(2)}) async-start(bf16[1,4,96]{2,0,1:T(2,128)(2,1)} %all_to_all.44), calls=%async_computation.5 | async-start | bytes 4096 | tf_op jit(solution)/shard_map/all_to_all | solution.py:71
  151.0 11.0 %convert_bitcast_fusion = bf16[1,1024,4096]{2,1,0:T(8,128)(2,1)} fusion(bf16[384,4096]{1,0:T(8,128)(2,1)} %all-gather.3.cloned.1.call-done, f32[384]{0:T(512)S(1)} %reshape.112, f32[384,1024]{1,0:T(8,128)} %fusion.6, f32[384,1024]{1,0:T(8,128)} %fusion.2), kind=kOutput, calls=%fused_computation.16 | convolution fusion | flops 3228172288 | bytes 14681600 | tf_op jit(solution)/shard_map/dot_general | solution.py:8
  162.0 6.9 %convert_bitcast_fusion.1 = bf16[1,4096,1024]{2,1,0:T(8,128)(2,1)} fusion(bf16[384,4096]{1,0:T(8,128)(2,1)S(1)} %copy-done.3, bf16[384,1024]{1,0:T(8,128)(2,1)S(1)} %copy-done.5), kind=kOutput, calls=%fused_computation.17 | convolution fusion | flops 3225419776 | bytes 12320768 | tf_op jit(solution)/shard_map/dot_general | solution.py:8
  168.9 25.4 %reduce-scatter.2.cloned.1.call-done = f32[512,384]{0,1:T(8,128)} async-done(((f32[4096,384]{0,1:T(8,128)}), f32[512,384]{0,1:T(8,128)}) %reduce-scatter.2.cloned.1.call-update) | async-done | bytes 786448 | tf_op jit(solution)/shard_map/reduce_scatter | solution.py:62
  194.3 1.9 convert_element_type.59
  196.2 4.6 %all-to-all-start.3 = ((bf16[512,4,96]{0,2,1:T(8,128)(2,1)}), bf16[512,4,96]{0,2,1:T(8,128)(2,1)S(1)}, u32[]{:S(2)}, u32[]{:S(2)}) async-start(bf16[512,4,96]{0,2,1:T(8,128)(2,1)} %bitcast.12), calls=%async_computation.4 | async-start | bytes 786432 | tf_op jit(solution)/shard_map/all_to_all | solution.py:70
  200.8 10.1 %convert_bitcast_fusion.2 = bf16[1,4096,1024]{2,1,0:T(8,128)(2,1)} fusion(bf16[384,4096]{1,0:T(8,128)(2,1)} %all-gather.5.cloned.1.call-done, bf16[384,1024]{1,0:T(8,128)(2,1)} %copy-done.6), kind=kOutput, calls=%fused_computation.18 | convolution fusion | flops 3225419776 | bytes 12320768 | tf_op jit(solution)/shard_map/dot_general | solution.py:8
  211.0 1.9 gather_fusion.4
  215.0 1.3 fusion.15
  (63 shorter events, 7.5 us)
Async XLA Ops:
  7.2 8.2 %copy-start = (bf16[128,512]{1,0:T(8,128)(2,1)S(1)}, bf16[128,512]{1,0:T(8,128)(2,1)}, u32[]{:S(2)}) copy-start(bf16[128,512]{1,0:T(8,128)(2,1)} %param.7) | copy-start | bytes 393220
  7.2 10.3 %copy-start.2 = (bf16[128,512]{1,0:T(8,128)(2,1)S(1)}, bf16[128,512]{1,0:T(8,128)(2,1)}, u32[]{:S(2)}) copy-start(bf16[128,512]{1,0:T(8,128)(2,1)} %param.8) | copy-start | bytes 393220
  7.2 62.4 %all-gather.5.cloned.1.call-start = ((), (), s32[]{:S(2)}) async-start(), calls=%async_computation.7 | async-start | bytes 3538944 | tf_op jit(solution)/shard_map/all_gather | solution.py:41
  37.6 66.6 %all-gather.3.cloned.1.call-start = ((), (), s32[]{:S(2)}) async-start(), calls=%async_computation.6 | async-start | bytes 3538944 | tf_op jit(solution)/shard_map/all_gather | solution.py:42
  51.6 142.6 %reduce-scatter.2.cloned.1.call-start = ((), (), s32[]{:S(2)}) async-start(), calls=%async_computation.8 | async-start | bytes 7077888 | tf_op jit(solution)/shard_map/reduce_scatter | solution.py:62
  69.6 9.0 %copy-start.3 = (bf16[384,4096]{1,0:T(8,128)(2,1)S(1)}, bf16[384,4096]{1,0:T(8,128)(2,1)}, u32[]{:S(2)}) copy-start(bf16[384,4096]{1,0:T(8,128)(2,1)} %all-gather.5.cloned.1.call-done) | copy-start | bytes 9437188
  104.2 20.9 %slice-start = ((s8[8388608]{0:T(1024)(128)(4,1)}), s8[4194304]{0:T(1024)(128)(4,1)S(1)}, s32[]{:S(2)}) async-start(s8[8388608]{0:T(1024)(128)(4,1)} %bitcast.78), calls=%async_computation.9 | async-start | bytes 8388608
  113.6 11.5 %copy-start.6 = (bf16[384,1024]{1,0:T(8,128)(2,1)}, bf16[384,1024]{1,0:T(8,128)(2,1)S(1)}, u32[]{:S(2)}) copy-start(bf16[384,1024]{1,0:T(8,128)(2,1)S(1)} %get-tuple-element.25) | copy-start | bytes 2359300
  113.6 11.5 %copy-start.4 = (bf16[384,1024]{1,0:T(8,128)(2,1)}, bf16[384,1024]{1,0:T(8,128)(2,1)S(1)}, u32[]{:S(2)}) copy-start(bf16[384,1024]{1,0:T(8,128)(2,1)S(1)} %get-tuple-element.26) | copy-start | bytes 2359300
  113.7 11.5 %slice-start.1 = ((s8[8388608]{0:T(1024)(128)(4,1)}), s8[4194304]{0:T(1024)(128)(4,1)S(1)}, s32[]{:S(2)}) async-start(s8[8388608]{0:T(1024)(128)(4,1)} %bitcast.78), calls=%async_computation.10 | async-start | bytes 8388608
  146.4 49.8 %all-to-all-start.4 = ((bf16[1,4,96]{2,0,1:T(2,128)(2,1)}), bf16[1,4,96]{2,0,1:T(2,128)(2,1)S(1)}, u32[]{:S(2)}, u32[]{:S(2)}) async-start(bf16[1,4,96]{2,0,1:T(2,128)(2,1)} %all_to_all.44), calls=%async_computation.5 | async-start | bytes 4096 | tf_op jit(solution)/shard_map/all_to_all | solution.py:71
  151.0 11.0 %copy-start.5 = (bf16[384,1024]{1,0:T(8,128)(2,1)S(1)}, bf16[384,1024]{1,0:T(8,128)(2,1)}, u32[]{:S(2)}) copy-start(bf16[384,1024]{1,0:T(8,128)(2,1)} %copy-done.4) | copy-start | bytes 2359300
  196.2 17.5 %all-to-all-start.3 = ((bf16[512,4,96]{0,2,1:T(8,128)(2,1)}), bf16[512,4,96]{0,2,1:T(8,128)(2,1)S(1)}, u32[]{:S(2)}, u32[]{:S(2)}) async-start(bf16[512,4,96]{0,2,1:T(8,128)(2,1)} %bitcast.12), calls=%async_computation.4 | async-start | bytes 786432 | tf_op jit(solution)/shard_map/all_to_all | solution.py:70
  200.8 15.5 %copy-start.1 = (bf16[128,512]{1,0:T(8,128)(2,1)S(1)}, bf16[128,512]{1,0:T(8,128)(2,1)}, u32[]{:S(2)}) copy-start(bf16[128,512]{1,0:T(8,128)(2,1)} %param.7) | copy-start | bytes 393220
Sparse Core Ops, SparseCore 0:
  37.7 31.8 all-gather.4
  71.5 32.7 all-gather.2
  132.6 61.6 reduce-scatter.1
where the time goes:
time: 223 us
  matrix products  72.3 us (32%)
  waiting for transfers between devices  53.5 us (24%)
  blocking collectives  53.1 us (24%)
  local copies, waits for them, and re-layouts  15.8 us (7%)
  between operations  14 us (6%)
  starting transfers between devices  9.3 us (4%)
  other arithmetic  4.84 us (2%)
    dot_general x8, matrix products, contract(): lax.dot_general(left, right, (((left_dim,), (right_dim,)), ((), ())), pre...  72.3 us
    reduce_scatter x1, waiting for transfers between devices, per_device(): lax.psum_scatter(contract(gate_w, gate_delta, 1, 1) + contract(up_w, up_d...  25.4 us
    all_gather x1, waiting for transfers between devices, per_device(): lax.all_gather(slice_grad, 'hid', axis=1, tiled=True)  18.5 us
    all_to_all x1, blocking collectives, per_device(): lax.all_to_all(pack(tokens), 'tok', split_axis=0, concat_axis=0, tiled=True)  17.9 us
    all_to_all x1, blocking collectives, per_device(): lax.all_to_all(pack(out_grad), 'tok', split_axis=0, concat_axis=0, tiled=...  13.9 us
    psum x1, blocking collectives, per_device(): route_total = lax.psum(route_local, 'hid')  13.1 us
    all_gather x1, waiting for transfers between devices, per_device(): lax.all_gather(slice_in, 'hid', axis=1, tiled=True)  9.63 us
    all_to_all x1, blocking collectives, per_device(): lax.all_to_all(slot_weight, 'tok', split_axis=0, concat_axis=0, tiled=True)  8.09 us
  transfers between devices with their start and end apart: 5, of which 3 were waited for; matrix products, arithmetic and copies ran while one was open for 22% of the time, Pallas kernels for 0%

commit v1 on v0

v1 whole, which is shorter than its diff:
```python
import jax
import jax.numpy as jnp
from jax import lax
from jax.experimental import pallas as pl
from jax.experimental.pallas import tpu as pltpu
from jax.sharding import PartitionSpec as P


def flip(index, relative, bits):
    for b in range(bits):
        if (relative >> b) & 1:
            index = index + (1 << b) - 2 * (1 << b) * ((index // (1 << b)) % 2)
    return index


def spread_kernel(bits, count, *refs):
    sources, outs = refs[:count], refs[count:2 * count]
    send, recv, local = refs[2 * count:]
    me = lax.axis_index("hid")
    rows, width = sources[0].shape
    half = rows // 2
    barrier = pltpu.get_barrier_semaphore()
    for b in range(bits):
        pl.semaphore_signal(
            barrier, inc=1, device_id={"hid": flip(me, 1 << b, bits)}, device_id_type=pl.DeviceIdType.MESH
        )
    pl.semaphore_wait(barrier, bits)
    outer = list(range(1, bits))
    orders = (outer + [0], outer[::-1] + [0])

    def columns(block):
        return pl.ds(pl.multiple_of(block * width, width), width)

    own = []
    for a in range(count):
        copy = pltpu.make_async_copy(sources[a], outs[a].at[:, columns(me)], local.at[a])
        copy.start()
        own.append(copy)
    everything, pending = [], {}
    for step in range(bits):
        for a in range(count):
            for h in range(2):
                order = orders[h]
                held = [0]
                for b in order[:step]:
                    held = held + [d ^ (1 << b) for d in held]
                for copy in pending.pop((a, h), []):
                    copy.wait_recv()
                started = []
                partner = flip(me, 1 << order[step], bits)
                lines = pl.ds(h * half, half)
                for d in held:
                    block = flip(me, d, bits)
                    where = outs[a].at[lines, columns(block)]
                    what = sources[a].at[lines, :] if d == 0 else where
                    slot = (a * 2 + h) * (1 << bits) + len(held) + held.index(d)
                    copy = pltpu.make_async_remote_copy(
                        src_ref=what, dst_ref=where, send_sem=send.at[slot], recv_sem=recv.at[slot],
                        device_id={"hid": partner}, device_id_type=pl.DeviceIdType.MESH,
                    )
                    copy.start()
                    started.append(copy)
                pending[(a, h)] = started
                everything += started
    for started in pending.values():
        for copy in started:
            copy.wait_recv()
    for copy in everything:
        copy.wait_send()
    for copy in own:
        copy.wait()


def spread(number, *blocks):
    size = lax.axis_size("hid")
    bits = size.bit_length() - 1
    count = len(blocks)
    rows, width = blocks[0].shape
    whole = pl.BlockSpec(memory_space=pltpu.VMEM)
    slots = 2 * count * size
    return pl.pallas_call(
        lambda *refs: spread_kernel(bits, count, *refs),
        out_shape=[jax.ShapeDtypeStruct((rows, width * size), b.dtype) for b in blocks],
        in_specs=[whole] * count,
        out_specs=[whole] * count,
        scratch_shapes=[
            pltpu.SemaphoreType.DMA((slots,)),
            pltpu.SemaphoreType.DMA((slots,)),
            pltpu.SemaphoreType.DMA((count,)),
        ],
        compiler_params=pltpu.CompilerParams(
            collective_id=number, has_side_effects=True, vmem_limit_bytes=32 * 1024 * 1024
        ),
        cost_estimate=pl.CostEstimate(flops=20_000_000_000, bytes_accessed=4 * rows * width * size * count, transcendentals=0),
    )(*blocks)


def contract(left, right, left_dim, right_dim):
    return lax.dot_general(
        left, right, (((left_dim,), (right_dim,)), ((), ())), preferred_element_type=jnp.float32
    )


def per_device(tokens, out_grad, routing_ids, route_weights, gate_matrix, up_matrix, down_matrix):
    groups = lax.axis_size("tok")
    tok_rows = tokens.shape[0]
    capacity = 3 * tok_rows // groups
    flat = routing_ids.reshape(-1)
    choices = flat.shape[0]
    onehot = (flat[:, None] == jnp.arange(groups, dtype=jnp.int32)[None, :]).astype(jnp.int32)
    position = jnp.sum((jnp.cumsum(onehot, axis=0) - onehot) * onehot, axis=1)
    slots = flat * capacity + position
    table = jnp.arange(groups * capacity, dtype=jnp.int32)
    match = (table[:, None, None] == slots.reshape(tok_rows, 2)[None]).astype(jnp.bfloat16)
    named = match[:, :, 0] + match[:, :, 1]
    slot_weight = jnp.sum(match * route_weights[None], axis=(1, 2), dtype=jnp.float32)
    both = jnp.concatenate([tokens, out_grad], axis=1)
    packed = contract(named, both, 1, 0).astype(jnp.bfloat16)
    width = tokens.shape[1]
    tail = jnp.broadcast_to(slot_weight.astype(jnp.bfloat16)[:, None], (groups * capacity, 128))
    packed = jnp.concatenate([packed, tail], axis=1)
    moved = lax.all_to_all(packed, "tok", split_axis=0, concat_axis=0, tiled=True)
    slice_in, slice_grad, rows_weight = moved[:, :width], moved[:, width:2 * width], moved[:, 2 * width]
    rows_in, rows_grad = spread(1, slice_in, slice_grad)
    gate_w = gate_matrix[0]
    up_w = up_matrix[0]
    down_w = down_matrix[0]
    gate = contract(rows_in, gate_w, 1, 0)
    upper = contract(rows_in, up_w, 1, 0)
    sig = jax.nn.sigmoid(gate)
    act = gate * sig
    weight_col = rows_weight.astype(jnp.float32)[:, None]
    hidden = (act * upper).astype(jnp.bfloat16)
    scaled = (act * upper * weight_col).astype(jnp.bfloat16)
    back = contract(rows_grad, down_w, 1, 1)
    route_local = jnp.sum(hidden.astype(jnp.float32) * back, axis=1)
    back_scaled = back * weight_col
    up_delta = (back_scaled * act).astype(jnp.bfloat16)
    gate_delta = (back_scaled * upper * sig * (1.0 + gate * (1.0 - sig))).astype(jnp.bfloat16)
    gate_out = contract(rows_in, gate_delta, 0, 0).astype(jnp.bfloat16)
    up_out = contract(rows_in, up_delta, 0, 0).astype(jnp.bfloat16)
    down_out = contract(scaled, rows_grad, 0, 0).astype(jnp.bfloat16)
    shares = lax.psum_scatter(
        (contract(gate_w, gate_delta, 1, 1) + contract(up_w, up_delta, 1, 1)).astype(jnp.bfloat16),
        "hid",
        scatter_dimension=0,
        tiled=True,
    )
    route_total = lax.psum(route_local, "hid").astype(jnp.bfloat16)
    moved_back = jnp.concatenate(
        [shares, jnp.broadcast_to(route_total[None], (16, route_total.shape[0]))], axis=0
    )
    back_rows = lax.all_to_all(moved_back, "tok", split_axis=1, concat_axis=1, tiled=True)
    features = tokens.shape[1]
    input_grad = contract(named, back_rows[:features], 0, 1).astype(jnp.bfloat16)
    back_route = back_rows[features].astype(jnp.float32)
    route_grad = jnp.sum(match.astype(jnp.float32) * back_route[:, None, None], axis=0)
    route_grad = route_grad.astype(jnp.bfloat16)
    return (input_grad, route_grad, gate_out[None], up_out[None], down_out[None])


def solution(mesh):
    in_specs = (
        P("tok", "hid"),
        P("tok", "hid"),
        P("tok", None),
        P("tok", None),
        P("tok", None, "hid"),
        P("tok", None, "hid"),
        P("tok", "hid", None),
    )
    out_specs = (
        P("tok", "hid"),
        P("tok", None),
        P("tok", None, "hid"),
        P("tok", None, "hid"),
        P("tok", "hid", None),
    )
    return jax.shard_map(
        per_device, mesh=mesh, in_specs=in_specs, out_specs=out_specs, check_vma=False
    )
```

time: 223 us -> 178 us (0.80)
  waiting for transfers between devices: 53.5 us -> 17.5 us
  Pallas kernels: 0 us -> 31.9 us
  local copies, waits for them, and re-layouts: 15.8 us -> 2 us
  matrix products: 72.3 us -> 59.6 us
  blocking collectives: 53.1 us -> 41.6 us
  starting transfers between devices: 9.3 us -> 4.63 us
    pallas_call x0 -> x1, Pallas kernels: none -> 31.9 us  [spread(): pl.pallas_call(lambda *refs: spread_kernel(bits, count, *refs), out_shape...]
    all_gather x2 -> x0, waiting for transfers between devices: 28.1 us -> none  [the longest x1 18.5 us: per_device(): lax.all_gather(slice_grad, 'hid', axis=1, tiled=True)]
    dot_general x8 -> x10, matrix products: 72.3 us -> 59.6 us  [contract(): lax.dot_general(left, right, (((left_dim,), (right_dim,)), ((), ())), pre...]
    all_to_all x3 -> x1, blocking collectives: 40 us -> 28.4 us  [per_device(): lax.all_to_all(packed, 'tok', split_axis=0, concat_axis=0, tiled=True)]
    reduce_scatter x1, waiting for transfers between devices: 25.4 us -> 13.9 us  [per_device(): lax.psum_scatter((contract(gate_w, gate_delta, 1, 1) + contract(up_w, up_...]
    gather x7 -> x0, local copies, waits for them, and re-layouts: 10.2 us -> none  [the longest x2 4.12 us: pack(): return jnp.where(valid[:, None], rows[token_row], jnp.zeros((), rows.dtype))]
    all_to_all x2 -> x1, starting transfers between devices: 9.18 us -> 4.59 us  [per_device(): lax.all_to_all(moved_back, 'tok', split_axis=1, concat_axis=1, tiled=True)]
    all_to_all x2 -> x1, waiting for transfers between devices: 0.01 us -> 3.59 us  [per_device(): lax.all_to_all(moved_back, 'tok', split_axis=1, concat_axis=1, tiled=True)]
  transfers between devices with their start and end apart: 5 -> 2, of which waited for: 3 -> 2; matrix products, arithmetic and copies ran while one was open for 22% -> 15% of each run, Pallas kernels for 0% -> 0%
where the time goes in v1:
time: 178 us; the launch traced here: 177 us
  matrix products  59.6 us (33%)
  blocking collectives  41.6 us (23%)
  Pallas kernels  31.9 us (18%)
  waiting for transfers between devices  17.5 us (10%)
  between operations  14.2 us (8%)
  other arithmetic  5.7 us (3%)
  starting transfers between devices  4.63 us (3%)
  local copies, waits for them, and re-layouts  2 us (1%)
    dot_general x10, matrix products, contract(): lax.dot_general(left, right, (((left_dim,), (right_dim,)), ((), ())), pre...  59.6 us
    pallas_call x1, Pallas kernels, spread(): pl.pallas_call(lambda *refs: spread_kernel(bits, count, *refs), out_shape...  31.9 us
    all_to_all x1, blocking collectives, per_device(): lax.all_to_all(packed, 'tok', split_axis=0, concat_axis=0, tiled=True)  28.4 us
    reduce_scatter x1, waiting for transfers between devices, per_device(): lax.psum_scatter((contract(gate_w, gate_delta, 1, 1) + contract(up_w, up_...  13.9 us
    psum x1, blocking collectives, per_device(): route_total = lax.psum(route_local, 'hid').astype(jnp.bfloat16)  13.2 us
    all_to_all x1, starting transfers between devices, per_device(): lax.all_to_all(moved_back, 'tok', split_axis=1, concat_axis=1, tiled=True)  4.59 us
    all_to_all x1, waiting for transfers between devices, per_device(): lax.all_to_all(moved_back, 'tok', split_axis=1, concat_axis=1, tiled=True)  3.59 us
  transfers between devices with their start and end apart: 2, of which 2 were waited for; matrix products, arithmetic and copies ran while one was open for 15% of the time, Pallas kernels for 0%

profile of v1, /device:TPU:0, one launch (start us, length us, event | category | flops | bytes accessed | tf_op | source)
XLA Modules:
  0.0 177.2 jit_solution(12360919460852620894)
XLA Ops:
  7.2 0.8 copy.31
  8.1 0.1 eq.39
  8.3 1.2 reduce-window.6
  9.9 0.1 reduce_sum.42
  10.1 0.7 multiply_add_fusion
  10.9 0.8 fusion.23
  11.7 1.3 convolution_convert_fusion
  13.2 28.4 %all_to_all.21 = bf16[4,96,1152]{2,1,0:T(8,128)(2,1)S(1)} all-to-all(bf16[4,96,1152]{2,1,0:T(8,128)(2,1)S(1)} %bitcast.67), channel_id=1, replica_groups=mesh['tok'=4,'hid'=8] {'tok'}, dimensions={0} | all-to-all | bytes 1769472 | tf_op jit(solution)/shard_map/all_to_all | solution.py:122
  41.9 31.9 %shard_map.110 = (bf16[384,4096]{1,0:T(8,128)(2,1)S(1)}, bf16[384,4096]{1,0:T(8,128)(2,1)S(1)}) custom-call(bf16[384,512]{1,0:T(8,128)(2,1)S(1)} %get-tuple-element.13.refs_0_, bf16[384,512]{1,0:T(8,128)(2,1)S(1)} %get-tuple-element.12.refs_1_), custom_call_target="tpu_custom_call" | custom-call | flops 20000000000 | bytes 12582912 | tf_op jit(solution)/shard_map/pallas_call | solution.py:81
  73.8 4.6 %fusion.6 = f32[384,1024]{1,0:T(8,128)} fusion(bf16[384,4096]{1,0:T(8,128)(2,1)S(1)} %get-tuple-element.8, bf16[1,4096,1024]{2,1,0:T(8,128)(2,1)S(1)} %bitcast.75), kind=kOutput, calls=%fused_computation.6 | convolution fusion | flops 3221225472 | bytes 13107200 | tf_op jit(solution)/shard_map/dot_general | solution.py:99
  78.4 4.6 %fusion.8 = f32[384,1024]{1,0:T(8,128)} fusion(bf16[384,4096]{1,0:T(8,128)(2,1)S(1)} %get-tuple-element.7, bf16[1,1024,4096]{2,1,0:T(8,128)(2,1)S(1)} %bitcast.71), kind=kOutput, calls=%fused_computation.8 | convolution fusion | flops 3221225472 | bytes 13107200 | tf_op jit(solution)/shard_map/dot_general | solution.py:99
  83.0 6.8 %multiply_convert_fusion.2 = (bf16[384,1024]{1,0:T(8,128)(2,1)S(1)}, f32[384]{0:T(512)S(1)}, bf16[384,1024]{1,0:T(8,128)(2,1)S(1)}, f32[384,1024]{1,0:T(8,128)}) fusion(f32[384,1024]{1,0:T(8,128)S(1)} %copy-done.1, f32[384,1024]{1,0:T(8,128)} %fusion.8, f32[384]{0:T(512)S(1)} %convert_reduce_fusion.1, bf16[384,4096]{1,0:T(8,128)(2,1)S(1)} %get-tuple-element.8, ...), kind=kOutput, calls=%fused_computation.18 | convolution fusion | flops 3228696064 | bytes 17828864 | tf_op jit(solution)/shard_map/dot_general | solution.py:99
  89.8 3.6 %fusion = f32[384,4096]{1,0:T(8,128)S(1)} fusion(bf16[384,1024]{1,0:T(8,128)(2,1)S(1)} %get-tuple-element.9, bf16[1,4096,1024]{2,1,0:T(8,128)(2,1)S(1)} %bitcast.73), kind=kOutput, calls=%fused_computation | convolution fusion | flops 3221225472 | bytes 15466496 | tf_op jit(solution)/shard_map/dot_general | solution.py:99
  93.5 10.4 %fusion.12 = bf16[4096,384]{0,1:T(8,128)(2,1)} fusion(f32[384,4096]{1,0:T(8,128)S(1)} %fusion, bf16[384,1024]{1,0:T(8,128)(2,1)S(1)} %get-tuple-element.11, bf16[1,4096,1024]{2,1,0:T(8,128)(2,1)} %param.12), kind=kOutput, calls=%fused_computation.14 | convolution fusion | flops 3224371200 | bytes 18612224 | tf_op jit(solution)/shard_map/dot_general | solution.py:99
  103.8 13.2 %psum.7 = bf16[384]{0:T(512)(128)(2,1)S(1)} all-reduce(f32[384]{0:T(512)S(1)} %get-tuple-element.10), channel_id=1, replica_groups=mesh['tok'=4,'hid'=8] {'hid'}, use_global_device_ids=true, to_apply=%region_6.7 | all-reduce | flops 384 | bytes 2304 | tf_op jit(solution)/shard_map/psum | solution.py:149
  117.1 10.2 %convert_bitcast_fusion.1 = bf16[1,4096,1024]{2,1,0:T(8,128)(2,1)} fusion(bf16[384,4096]{1,0:T(8,128)(2,1)} %copy-done, bf16[384,1024]{1,0:T(8,128)(2,1)} %copy-done.4), kind=kOutput, calls=%fused_computation.11 | convolution fusion | flops 3225419776 | bytes 12320768 | tf_op jit(solution)/shard_map/dot_general | solution.py:99
  127.3 7.2 %convert_bitcast_fusion = bf16[1,1024,4096]{2,1,0:T(8,128)(2,1)} fusion(bf16[384,4096]{1,0:T(8,128)(2,1)S(1)} %get-tuple-element.7, f32[384]{0:T(512)S(1)} %convert_reduce_fusion.1, f32[384,1024]{1,0:T(8,128)S(1)} %copy-done.2, f32[384,1024]{1,0:T(8,128)S(1)} %copy-done.3), kind=kOutput, calls=%fused_computation.10 | convolution fusion | flops 3228172288 | bytes 14681600 | tf_op jit(solution)/shard_map/dot_general | solution.py:99
  134.5 13.9 %reduce-scatter.2.cloned.1.call-done = bf16[512,384]{0,1:T(8,128)(2,1)} async-done(((bf16[4096,384]{0,1:T(8,128)(2,1)}), bf16[512,384]{0,1:T(8,128)(2,1)}) %reduce-scatter.2.cloned.1.call-update) | async-done | bytes 393232 | tf_op jit(solution)/shard_map/reduce_scatter | solution.py:143
  148.5 1.8 %pad_maximum_fusion.1 = bf16[528,384]{0,1:T(8,128)(2,1)} fusion(bf16[16,384]{0,1:T(8,128)(2,1)S(1)} %broadcast_in_dim.11, bf16[512,384]{0,1:T(8,128)(2,1)} %reduce-scatter.2.cloned.1.call-done), kind=kLoop, calls=%fused_computation.26 | loop fusion | flops 811008 | bytes 811008 | tf_op jit(solution)/shard_map/concatenate | solution.py:150
  150.3 4.6 %all-to-all-start.1 = ((bf16[528,4,96]{0,2,1:T(8,128)(2,1)}), bf16[528,4,96]{0,2,1:T(8,128)(2,1)S(1)}, u32[]{:S(2)}, u32[]{:S(2)}) async-start(bf16[528,4,96]{0,2,1:T(8,128)(2,1)} %bitcast.9), calls=%async_computation.2 | async-start | bytes 983040 | tf_op jit(solution)/shard_map/all_to_all | solution.py:153
  154.9 10.0 %convert_bitcast_fusion.2 = bf16[1,4096,1024]{2,1,0:T(8,128)(2,1)} fusion(bf16[384,4096]{1,0:T(8,128)(2,1)} %copy-done, bf16[384,1024]{1,0:T(8,128)(2,1)} %copy-done.5), kind=kOutput, calls=%fused_computation.12 | convolution fusion | flops 3225419776 | bytes 12320768 | tf_op jit(solution)/shard_map/dot_general | solution.py:99
  164.9 3.6 %all-to-all-done.1 = bf16[528,4,96]{0,2,1:T(8,128)(2,1)S(1)} async-done(((bf16[528,4,96]{0,2,1:T(8,128)(2,1)}), bf16[528,4,96]{0,2,1:T(8,128)(2,1)S(1)}, u32[]{:S(2)}, u32[]{:S(2)}) %all-to-all-start.1) | async-done | bytes 405536 | tf_op jit(solution)/shard_map/all_to_all | solution.py:153
  168.6 0.9 convolution_convert_fusion.1
  169.7 0.7 multiply_reduce_fusion.1
  (48 shorter events, 1.5 us)
Async XLA Ops:
  7.2 141.2 %reduce-scatter.2.cloned.1.call-start = ((), (), s32[]{:S(2)}) async-start(), calls=%async_computation.3 | async-start | bytes 3538944 | tf_op jit(solution)/shard_map/reduce_scatter | solution.py:143
  41.7 32.0 %slice-start.4 = ((s8[8388608]{0:T(1024)(128)(4,1)}), s8[4194304]{0:T(1024)(128)(4,1)S(1)}, s32[]{:S(2)}) async-start(s8[8388608]{0:T(1024)(128)(4,1)} %bitcast.74), calls=%async_computation.8 | async-start | bytes 8388608
  41.7 36.6 %slice-start = ((s8[8388608]{0:T(1024)(128)(4,1)}), s8[4194304]{0:T(1024)(128)(4,1)S(1)}, s32[]{:S(2)}) async-start(s8[8388608]{0:T(1024)(128)(4,1)} %bitcast.70), calls=%async_computation.4 | async-start | bytes 8388608
  41.7 41.2 %slice-start.2 = ((s8[8388608]{0:T(1024)(128)(4,1)}), s8[4194304]{0:T(1024)(128)(4,1)S(1)}, s32[]{:S(2)}) async-start(s8[8388608]{0:T(1024)(128)(4,1)} %bitcast.72), calls=%async_computation.6 | async-start | bytes 8388608
  41.8 31.9 %slice-start.5 = ((s8[8388608]{0:T(1024)(128)(4,1)}), s8[4194304]{0:T(1024)(128)(4,1)S(1)}, s32[]{:S(2)}) async-start(s8[8388608]{0:T(1024)(128)(4,1)} %bitcast.74), calls=%async_computation.9 | async-start | bytes 8388608
  41.8 36.5 %slice-start.1 = ((s8[8388608]{0:T(1024)(128)(4,1)}), s8[4194304]{0:T(1024)(128)(4,1)S(1)}, s32[]{:S(2)}) async-start(s8[8388608]{0:T(1024)(128)(4,1)} %bitcast.70), calls=%async_computation.5 | async-start | bytes 8388608
  41.8 41.1 %slice-start.3 = ((s8[8388608]{0:T(1024)(128)(4,1)}), s8[4194304]{0:T(1024)(128)(4,1)S(1)}, s32[]{:S(2)}) async-start(s8[8388608]{0:T(1024)(128)(4,1)} %bitcast.72), calls=%async_computation.7 | async-start | bytes 8388608
  73.7 9.3 %copy-start = (bf16[384,4096]{1,0:T(8,128)(2,1)}, bf16[384,4096]{1,0:T(8,128)(2,1)S(1)}, u32[]{:S(2)}) copy-start(bf16[384,4096]{1,0:T(8,128)(2,1)S(1)} %get-tuple-element.8) | copy-start | bytes 9437188
  78.4 4.6 %copy-start.1 = (f32[384,1024]{1,0:T(8,128)S(1)}, f32[384,1024]{1,0:T(8,128)}, u32[]{:S(2)}) copy-start(f32[384,1024]{1,0:T(8,128)} %fusion.6) | copy-start | bytes 4718596
  89.8 3.7 %copy-start.5 = (bf16[384,1024]{1,0:T(8,128)(2,1)}, bf16[384,1024]{1,0:T(8,128)(2,1)S(1)}, u32[]{:S(2)}) copy-start(bf16[384,1024]{1,0:T(8,128)(2,1)S(1)} %get-tuple-element.9) | copy-start | bytes 2359300
  89.8 3.7 %copy-start.4 = (bf16[384,1024]{1,0:T(8,128)(2,1)}, bf16[384,1024]{1,0:T(8,128)(2,1)S(1)}, u32[]{:S(2)}) copy-start(bf16[384,1024]{1,0:T(8,128)(2,1)S(1)} %get-tuple-element.11) | copy-start | bytes 2359300
  117.1 10.2 %copy-start.2 = (f32[384,1024]{1,0:T(8,128)S(1)}, f32[384,1024]{1,0:T(8,128)}, u32[]{:S(2)}) copy-start(f32[384,1024]{1,0:T(8,128)} %fusion.6) | copy-start | bytes 4718596
  117.1 10.2 %copy-start.3 = (f32[384,1024]{1,0:T(8,128)S(1)}, f32[384,1024]{1,0:T(8,128)}, u32[]{:S(2)}) copy-start(f32[384,1024]{1,0:T(8,128)} %get-tuple-element.14) | copy-start | bytes 4718596
  150.3 18.2 %all-to-all-start.1 = ((bf16[528,4,96]{0,2,1:T(8,128)(2,1)}), bf16[528,4,96]{0,2,1:T(8,128)(2,1)S(1)}, u32[]{:S(2)}, u32[]{:S(2)}) async-start(bf16[528,4,96]{0,2,1:T(8,128)(2,1)} %bitcast.9), calls=%async_computation.2 | async-start | bytes 983040 | tf_op jit(solution)/shard_map/all_to_all | solution.py:153
Sparse Core Ops, SparseCore 0:
  104.0 44.3 reduce-scatter.1
